TPU v7x, 32 devices: a whole 2x2x4 slice. The times are simulated.
32 devices in a mesh: chan: 8 (over y, x, core), tm: 4 (over z).
Axes of the slice: x: 2, y: 2, z: 4, core: 2. Of those that a mesh axis runs over, the one named last changes fastest.
Arguments:
- record: bfloat16 [128, 2048], P('chan', 'tm'), may hold values from -6 to 6
- tail: bfloat16 [128, 255], P('chan'), may hold values from -6 to 6
- templates: bfloat16 [128, 128, 128], P(None, 'chan'), may hold values from -6 to 6
- shifts: int32 [128, 128], P(None, 'chan'), may hold values from 0 to 127
- mask: int32 [128], P('chan'), may hold values 0 or 1
Outputs:
- stack: float32 [128, 2048], P('chan', 'tm')
All inputs are finite; a program needn't handle non-finite values. No bound on the sum of `mask` on one device may be relied on, other than what follows from the above.
Results may differ from a plain program's by a relative error of at most 0.0029.
Values may be sent and summed in bfloat16 or wider, within the bound.
A program may use at most 64 MiB of HBM per device.

v0:
```python
import jax
import jax.numpy as jnp
from jax import lax
from jax.sharding import PartitionSpec as P


def passed_along(block, axis, distance):
    devices = range(lax.axis_size(axis))
    route = [(i - distance, i) for i in devices if i - distance in devices]
    return lax.ppermute(block, axis, route)


def unit_templates(templates):
    values = templates.astype(jnp.float32)
    tap_count = templates.shape[2]
    centered = values - jnp.mean(values, axis=2, keepdims=True)
    norm = jnp.sqrt(tap_count * (jnp.mean(centered * centered, axis=2, keepdims=True) + 1e-06))
    return (centered / norm).astype(jnp.bfloat16)


def window_spread(samples, tap_count):
    values = samples.astype(jnp.float32)
    zero = jnp.zeros((values.shape[0], 1), jnp.float32)
    sums = jnp.concatenate([zero, jnp.cumsum(values, axis=1)], axis=1)
    squares = jnp.concatenate([zero, jnp.cumsum(values * values, axis=1)], axis=1)
    window = sums[:, tap_count:] - sums[:, :-tap_count]
    power = squares[:, tap_count:] - squares[:, :-tap_count]
    return jnp.sqrt(power - window * window / tap_count + tap_count * 1e-06)


def align_lags(normed, shift_rows, out_len):
    shift_range = normed.shape[2] - out_len
    bit_count = max(shift_range - 1, 0).bit_length()
    needed = out_len + (1 << bit_count) - 1
    current = normed
    if needed > current.shape[2]:
        current = jnp.pad(current, ((0, 0), (0, 0), (0, needed - current.shape[2])))
    for position in range(bit_count):
        offset = 1 << position
        kept_len = current.shape[2] - offset
        chosen = (shift_rows >> position & 1)[:, :, None] == 1
        current = jnp.where(chosen, current[:, :, offset:], current[:, :, :kept_len])
    return current[:, :, :out_len]


def channel_terms(ext_rows, unit_rows, shift_rows, mask_rows, out_len):
    tap_count = unit_rows.shape[2]
    chan_count = ext_rows.shape[0]
    templ_count = unit_rows.shape[0]
    filters = jnp.transpose(unit_rows, (1, 0, 2)).reshape(chan_count * templ_count, 1, tap_count)
    grouped = lax.conv_general_dilated(
        ext_rows[None, :, :],
        filters,
        (1,),
        "VALID",
        feature_group_count=chan_count,
        preferred_element_type=jnp.float32,
    )[0]
    lag_count = grouped.shape[1]
    product = jnp.transpose(grouped.reshape(chan_count, templ_count, lag_count), (1, 0, 2))
    spread = window_spread(ext_rows, tap_count)
    normed = product / spread[None, :, :]
    aligned = align_lags(normed, shift_rows, out_len)
    return jnp.sum(aligned * mask_rows[None, :, None], axis=1)


def shards(record, tail, templates, shifts, mask):
    tap_count = templates.shape[2]
    out_len = record.shape[1]
    halo_len = tail.shape[1]
    incoming = passed_along(record[:, :halo_len], "tm", -1)
    at_end = lax.axis_index("tm") == lax.axis_size("tm") - 1
    extended = jnp.concatenate([record, jnp.where(at_end, tail, incoming)], axis=1)
    unit = unit_templates(templates)
    weights = mask.astype(jnp.float32)
    summed = lax.psum_scatter(
        channel_terms(extended, unit, shifts, weights, out_len),
        "chan",
        scatter_dimension=0,
        tiled=True,
    )
    total = lax.psum(jnp.sum(weights), "chan")
    return summed * jnp.sqrt(tap_count / jnp.maximum(total, 1.0))


def solution(mesh):
    in_specs = (P("chan", "tm"), P("chan", None), P(None, "chan", None), P(None, "chan"), P("chan"))
    out_specs = P("chan", "tm")
    return jax.shard_map(shards, mesh=mesh, in_specs=in_specs, out_specs=out_specs, check_vma=False)
```

profile of v0, /device:TPU:0, one launch (start us, length us, event | category | flops | bytes accessed | tf_op | source)
XLA Modules:
  0.0 127.4 jit_solution(14662429962662453873)
XLA Ops:
  6.5 0.0 copy-start.1
  6.5 0.0 reduce-scatter.4.cloned.1.call-start
  6.5 0.7 slice.80
  7.2 1.3 %collective-permute-start = (bf16[16,255]{1,0:T(8,128)(2,1)S(1)}, bf16[16,255]{1,0:T(8,128)(2,1)S(1)}, u32[]{:S(2)}, u32[]{:S(2)}) collective-permute-start(bf16[16,255]{1,0:T(8,128)(2,1)S(1)} %slice.80), channel_id=1, source_target_pairs={{1,0},{2,1},{3,2},{5,4},{6,5},{7,6},{9,8},{10,9},{11,10},{13,12},{... | collective-permute-start | bytes 24488 | tf_op jit(solution)/shard_map/ppermute | solution.py:10
  8.5 1.4 %convert_reduce_fusion = f32[128,16]{0,1:T(8,128)S(1)} fusion(bf16[128,16,128]{2,1,0:T(8,128)(2,1)} %param.7), kind=kLoop, calls=%fused_computation.16 | loop fusion | flops 522240 | bytes 532480 | tf_op jit(solution)/shard_map/reduce_sum | solution.py:16
  9.9 1.7 %fusion.9 = f32[128,16]{0,1:T(8,128)S(1)} fusion(f32[128,16]{0,1:T(8,128)S(1)} %broadcast_multiply_fusion.1, bf16[128,16,128]{2,1,0:T(8,128)(2,1)} %param.7), kind=kLoop, calls=%fused_computation.19 | loop fusion | flops 1046528 | bytes 540672 | tf_op jit(solution)/shard_map/reduce_sum | solution.py:17
  11.6 1.7 %fusion.10 = bf16[128,16,128]{2,0,1:T(8,128)(2,1)S(1)} fusion(f32[128,16]{0,1:T(8,128)S(1)} %multiply_sqrt_fusion, f32[128,16]{0,1:T(8,128)S(1)} %broadcast_multiply_fusion.1, bf16[128,16,128]{2,1,0:T(8,128)(2,1)} %param.7), kind=kLoop, calls=%fused_computation.20 | loop fusion | flops 1048576 | bytes 1064960 | tf_op jit(solution)/shard_map/convert_element_type | solution.py:18
  13.3 0.7 and_compare_fusion.6
  14.0 0.2 copy.46
  14.2 0.7 convert_element_type.15
  14.9 0.0 collective-permute-done
  14.9 0.7 fusion.18
  15.6 0.7 fusion.20
  16.4 1.7 %reduce-window.16 = f32[16,6,128]{2,0,1:T(8,128)S(1)} reduce-window(f32[16,6,128]{2,0,1:T(8,128)S(1)} %copy_bitcast_fusion.2, f32[]{:T(128)} %constant.15.clone.1), window={size=1x1x128 pad=0_0x0_0x127_0}, to_apply=%region_4.5 | reduce-window | flops 1560576 | bytes 98308 | tf_op jit(solution)/shard_map/reduce-window.2
  18.1 0.2 slice_reduce_fusion
  18.3 1.7 %reduce-window.14 = f32[16,6,128]{2,0,1:T(8,128)S(1)} reduce-window(f32[16,6,128]{2,0,1:T(8,128)S(1)} %copy_bitcast_fusion.3, f32[]{:T(128)} %constant.15.clone.1), window={size=1x1x128 pad=0_0x0_0x127_0}, to_apply=%region_2.3 | reduce-window | flops 1560576 | bytes 98308 | tf_op jit(solution)/shard_map/reduce-window
  20.0 0.2 slice_reduce_fusion.1
  20.2 0.1 copy_bitcast_fusion
  20.3 0.1 fusion.14
  20.4 0.2 copy.52
  20.6 0.9 copy.47
  21.5 0.0 copy-done.1
  21.6 52.3 %fusion.1 = f32[1,2048,640]{1,0,2:T(1,128)S(1)} fusion(bf16[1,16,767]{1,0,2:T(2,128)(2,1)S(1)} %copy.47, s32[2048]{0:T(1024)S(1)} %copy-done.1, bf16[2048,128]{0,1:T(8,128)(2,1)S(1)} %copy.46), kind=kOutput, calls=%fused_computation.2 | convolution fusion | flops 5377097728 | bytes 5799904 | tf_op jit(solution)/shard_map/conv_general_dilated | solution.py:51
  73.8 1.9 %divide_bitcast_fusion = f32[128,16,640]{0,1,2:T(8,128)S(1)} fusion(f32[16,128,640]{1,0,2:T(8,128)S(1)} %bitcast.34, f32[16,640]{0,1:T(8,128)S(1)} %copy.52), kind=kLoop, calls=%fused_computation.3 | loop fusion | flops 1310720 | bytes 10526720 | tf_op jit(solution)/shard_map/div | solution.py:62
  75.8 0.3 slice_select_fusion
  76.1 0.3 slice_select_fusion.1
  76.5 0.3 slice_select_fusion.2
  76.8 0.3 slice_select_fusion.3
  77.2 0.3 slice_select_fusion.4
  77.5 0.3 slice_select_fusion.5
  77.8 0.6 fusion.22
  78.4 0.0 copy-start
  78.4 1.6 %fusion.4 = f32[128,512]{0,1:T(8,128)S(1)} fusion(f32[128,16,513]{0,1,2:T(8,128)S(1)} %get-tuple-element.6, f32[128,16,513]{0,1,2:T(8,128)S(1)} %get-tuple-element.5, f32[16]{0:T(128)S(1)} %convert_element_type.15, pred[128,16]{0,1:T(8,128)(4,1)S(1)} %get-tuple-element.9), kind=kLoop, calls=%fused_computation.12 | loop fusion | flops 3080192 | bytes 8652864 | tf_op jit(solution)/shard_map/reduce_sum | solution.py:64
  80.1 0.8 copy.54
  80.9 0.0 reduce-scatter.4.cloned.1.call-update
  80.9 0.0 copy-done
  80.9 0.6 convert_reduce_fusion.1
  81.5 15.8 %psum.7 = f32[]{:T(128)} all-reduce(f32[]{:T(128)} %convert_reduce_fusion.1), channel_id=1, replica_groups=mesh['chan'=8,'tm'=4] {'chan'}, use_global_device_ids=true, to_apply=%region_9.10 | all-reduce | flops 1 | bytes 8 | tf_op jit(solution)/shard_map/psum | solution.py:82
  98.0 21.2 %reduce-scatter.4.cloned.1.call-done = f32[16,512]{1,0:T(8,128)} async-done(((f32[128,512]{1,0:T(8,128)}), f32[16,512]{1,0:T(8,128)}) %reduce-scatter.4.cloned.1.call-update) | async-done | bytes 32784 | tf_op jit(solution)/shard_map/reduce_scatter | solution.py:76
  119.2 1.4 %broadcast_multiply_fusion = f32[16,512]{1,0:T(8,128)} fusion(f32[16,512]{1,0:T(8,128)} %reduce-scatter.4.cloned.1.call-done, f32[]{:T(128)S(6)} %sqrt.16), kind=kLoop, calls=%fused_computation.41 | loop fusion | flops 8192 | bytes 65540 | tf_op jit(solution)/shard_map/mul | solution.py:83
  (7 shorter events, 0.1 us)
Async XLA Ops:
  6.5 15.0 %copy-start.1 = (s32[2048]{0:T(1024)S(1)}, s32[2048]{0:T(1024)}, u32[]{:S(2)}) copy-start(s32[2048]{0:T(1024)} %constant.14.clone.1) | copy-start | bytes 24580
  6.5 112.7 %reduce-scatter.4.cloned.1.call-start = ((), (), s32[]{:S(2)}) async-start(), calls=%async_computation.1 | async-start | bytes 294912 | tf_op jit(solution)/shard_map/reduce_scatter | solution.py:76
  7.2 7.7 %collective-permute-start = (bf16[16,255]{1,0:T(8,128)(2,1)S(1)}, bf16[16,255]{1,0:T(8,128)(2,1)S(1)}, u32[]{:S(2)}, u32[]{:S(2)}) collective-permute-start(bf16[16,255]{1,0:T(8,128)(2,1)S(1)} %slice.80), channel_id=1, source_target_pairs={{1,0},{2,1},{3,2},{5,4},{6,5},{7,6},{9,8},{10,9},{11,10},{13,12},{... | collective-permute-start | bytes 24488 | tf_op jit(solution)/shard_map/ppermute | solution.py:10
  78.4 2.5 %copy-start = (s32[16]{0:T(128)S(1)}, s32[16]{0:T(128)}, u32[]{:S(2)}) copy-start(s32[16]{0:T(128)} %param.9) | copy-start | bytes 196
Sparse Core Ops, SparseCore 0:
  81.0 38.1 reduce-scatter.3
where the time goes:
time: 128 us; the launch traced here: 127 us
  matrix products  52.3 us (41%)
  waiting for transfers between devices  21.2 us (17%)
  other arithmetic  18.8 us (15%)
  blocking collectives  15.8 us (12%)
  between operations  14.3 us (11%)
  local copies, waits for them, and re-layouts  3.76 us (3%)
  starting transfers between devices  1.28 us (1%)
    conv_general_dilated x1, matrix products, channel_terms(): lax.conv_general_dilated(ext_rows[None, :, :], filters, (1,), 'VALID', fe...  52.3 us
    reduce_scatter x1, waiting for transfers between devices, shards(): lax.psum_scatter(channel_terms(extended, unit, shifts, weights, out_len),...  21.2 us
    psum x1, blocking collectives, shards(): total = lax.psum(jnp.sum(weights), 'chan')  15.8 us
    another operation x5, other arithmetic  3.59 us
  transfers between devices with their start and end apart: 2, of which 1 were waited for; matrix products, arithmetic and copies ran while one was open for 5% of the time, Pallas kernels for 0%

commit v1 on v0

v1 whole, which is shorter than its diff:
```python
import functools

import jax
import jax.numpy as jnp
from jax import lax
from jax.experimental import pallas as pl
from jax.experimental.pallas import tpu as pltpu
from jax.sharding import PartitionSpec as P

MESH = pl.DeviceIdType.MESH
LANES = 128
SUBLANES = 8
WIRE = jnp.float32


def ahead(values, distance):
    width = values.shape[1]
    distance = distance % width
    if distance == 0:
        return values
    return pltpu.roll(values, width - distance, 1)


def hankel(samples, tap_count, lag_count):
    width = samples.shape[1]
    rows = jnp.broadcast_to(samples, (SUBLANES, width))
    row = lax.broadcasted_iota(jnp.int32, (SUBLANES, width), 0)
    for bit in range(3):
        rows = jnp.where((row >> bit) & 1 == 1, ahead(rows, 1 << bit), rows)
    groups = [ahead(rows, start)[:, :lag_count] for start in range(0, tap_count, SUBLANES)]
    return jnp.concatenate(groups, axis=0).astype(jnp.bfloat16)


def kernel(n_chan, n_tm, record, tail, templates, shifts, mask, out, ext, halo, inverse, unit, normed,
           part, landed, tally, tallies, send_sem, recv_sem, tally_send, tally_recv, halo_send, halo_recv):
    chan = lax.axis_index("chan")
    tm = lax.axis_index("tm")
    chan_count, out_len = record.shape
    templ_count, _, tap_count = templates.shape
    halo_len = tail.shape[1]
    halo_width = halo.shape[1]
    lag_count = out_len + LANES
    rows = templ_count // n_chan

    barrier = pltpu.get_barrier_semaphore()
    for i in range(1, n_chan):
        pl.semaphore_signal(barrier, inc=1, device_id={"chan": lax.rem(chan + i, n_chan)}, device_id_type=MESH)

    @pl.when(tm > 0)
    def _():
        pl.semaphore_signal(barrier, inc=1, device_id={"tm": tm - 1}, device_id_type=MESH)

    @pl.when(tm < n_tm - 1)
    def _():
        pl.semaphore_signal(barrier, inc=1, device_id={"tm": tm + 1}, device_id_type=MESH)

    count = mask[0]
    for c in range(1, chan_count):
        count = count + mask[c]
    tally[...] = jnp.full(tally.shape, count, jnp.int32).astype(jnp.float32)
    ext[:, :out_len] = record[...].astype(jnp.float32)

    group = min(16, templ_count)

    def normalise(i, carry):
        values = templates[pl.ds(i * group, group)].astype(jnp.float32).reshape(group * chan_count, tap_count)
        centered = values - jnp.sum(values, axis=1, keepdims=True) * (1.0 / tap_count)
        power = jnp.sum(centered * centered, axis=1, keepdims=True) * (1.0 / tap_count)
        scale = 1.0 / jnp.sqrt(tap_count * (power + 1e-06))
        unit[pl.ds(pl.multiple_of(i * group * chan_count, SUBLANES), group * chan_count), :] = centered * scale
        return carry

    lax.fori_loop(0, templ_count // group, normalise, 0)

    neighbours = jnp.minimum(tm, 1) + jnp.minimum(n_tm - 1 - tm, 1)
    pl.semaphore_wait(barrier, n_chan - 1 + neighbours)

    halo_copy = pltpu.make_async_remote_copy(
        src_ref=record.at[:, pl.ds(0, halo_width)], dst_ref=halo, send_sem=halo_send, recv_sem=halo_recv,
        device_id={"tm": jnp.maximum(tm - 1, 0)}, device_id_type=MESH)

    def tally_copy(i):
        return pltpu.make_async_remote_copy(
            src_ref=tally, dst_ref=tallies.at[i], send_sem=tally_send.at[i], recv_sem=tally_recv.at[i],
            device_id={"chan": lax.rem(chan + i, n_chan)}, device_id_type=MESH)

    def part_copy(i):
        return pltpu.make_async_remote_copy(
            src_ref=part.at[i], dst_ref=landed.at[i], send_sem=send_sem.at[i], recv_sem=recv_sem.at[i],
            device_id={"chan": lax.rem(chan + i, n_chan)}, device_id_type=MESH)

    @pl.when(tm > 0)
    def _():
        halo_copy.start()

    for i in range(1, n_chan):
        tally_copy(i).start()

    @pl.when(tm < n_tm - 1)
    def _():
        halo_copy.wait_recv()
        ext[:, out_len:] = halo[...].astype(jnp.float32)

    @pl.when(tm == n_tm - 1)
    def _():
        ext[:, out_len:] = jnp.zeros((chan_count, halo_width), jnp.float32)
        ext[:, out_len:out_len + halo_len] = tail[...].astype(jnp.float32)

    sums = ext[...]
    squares = sums * sums
    for bit in range(tap_count.bit_length() - 1):
        sums = sums + ahead(sums, 1 << bit)
        squares = squares + ahead(squares, 1 << bit)
    window = sums[:, :lag_count]
    variance = jnp.maximum(squares[:, :lag_count] - window * window * (1.0 / tap_count), 0.0)
    inverse[...] = 1.0 / jnp.sqrt(variance + tap_count * 1e-06)

    def correlate(c, carry):
        taps = unit[pl.ds(c, templ_count, stride=chan_count), :].astype(jnp.bfloat16)
        product = jnp.dot(taps, hankel(ext[pl.ds(c, 1), :], tap_count, lag_count),
                          preferred_element_type=jnp.float32)
        weight = jnp.full((1, lag_count), mask[c], jnp.int32).astype(jnp.float32)
        normed[c] = product * (inverse[pl.ds(c, 1), :] * weight)
        return carry

    lax.fori_loop(0, chan_count, correlate, 0, unroll=4)

    def block_sum(block):
        place = pl.ds(pl.multiple_of(block * rows, SUBLANES), rows)
        moveouts = shifts[place, :]
        lane = lax.broadcasted_iota(jnp.int32, (rows, LANES), 1)
        tiles = out_len // LANES
        totals = [jnp.zeros((rows, LANES), jnp.float32)] * tiles
        for c in range(chan_count):
            position = lane + moveouts[:, c:c + 1]
            index = position & (LANES - 1)
            inside = position < LANES
            turned = [
                jnp.take_along_axis(normed[c, place, pl.ds(b * LANES, LANES)], index, axis=1,
                                    mode="promise_in_bounds")
                for b in range(tiles + 1)
            ]
            totals = [totals[b] + jnp.where(inside, turned[b], turned[b + 1]) for b in range(tiles)]
        return jnp.concatenate(totals, axis=1)

    def ship(i, carry):
        part[i] = block_sum(lax.rem(chan + i, n_chan)).astype(part.dtype)
        part_copy(i).start()
        return carry

    lax.fori_loop(1, n_chan, ship, 0)
    total = block_sum(chan)
    number = tally[...]
    for i in range(1, n_chan):
        tally_copy(i).wait_recv()
        number = number + tallies[i]
    scale = jnp.sqrt(tap_count / jnp.maximum(number[0:1, :], 1.0))
    for i in range(1, n_chan):
        part_copy(i).wait_recv()
        total = total + landed[i].astype(jnp.float32)
    for b in range(out_len // LANES):
        span = slice(b * LANES, (b + 1) * LANES)
        out[:, span] = total[:, span] * scale

    for i in range(1, n_chan):
        tally_copy(i).wait_send()
        part_copy(i).wait_send()

    @pl.when(tm > 0)
    def _():
        halo_copy.wait_send()


def shards(n_chan, n_tm, record, tail, templates, shifts, mask):
    chan_count, out_len = record.shape
    templ_count, _, tap_count = templates.shape
    halo_len = tail.shape[1]
    halo_width = -(-halo_len // LANES) * LANES
    lag_count = out_len + LANES
    rows = templ_count // n_chan
    assert tap_count == LANES and halo_len - tap_count < LANES and out_len % LANES == 0
    vmem = pl.BlockSpec(memory_space=pltpu.VMEM)
    f32 = jnp.float32
    dma = pltpu.SemaphoreType.DMA
    return pl.pallas_call(
        functools.partial(kernel, n_chan, n_tm),
        out_shape=jax.ShapeDtypeStruct((rows, out_len), f32),
        in_specs=[vmem, vmem, vmem, vmem, pl.BlockSpec(memory_space=pltpu.SMEM)],
        out_specs=vmem,
        scratch_shapes=[
            pltpu.VMEM((chan_count, out_len + halo_width), f32),
            pltpu.VMEM((chan_count, halo_width), record.dtype),
            pltpu.VMEM((chan_count, lag_count), f32),
            pltpu.VMEM((templ_count * chan_count, tap_count), f32),
            pltpu.VMEM((chan_count, templ_count, lag_count), f32),
            pltpu.VMEM((n_chan, rows, out_len), WIRE),
            pltpu.VMEM((n_chan, rows, out_len), WIRE),
            pltpu.VMEM((SUBLANES, LANES), f32),
            pltpu.VMEM((n_chan, SUBLANES, LANES), f32),
            dma((n_chan,)), dma((n_chan,)), dma((n_chan,)), dma((n_chan,)), dma, dma,
        ],
        compiler_params=pltpu.CompilerParams(collective_id=0, has_side_effects=True),
        name="matched_stack",
    )(record, tail, templates, shifts, mask)


def solution(mesh):
    in_specs = (P("chan", "tm"), P("chan", None), P(None, "chan", None), P(None, "chan"), P("chan"))
    body = functools.partial(shards, mesh.shape["chan"], mesh.shape["tm"])
    return jax.shard_map(body, mesh=mesh, in_specs=in_specs, out_specs=P("chan", "tm"), check_vma=False)
```

time: 128 us -> 26.1 us (0.20)
  the two profiles are of different devices: /device:TPU:0 before, /device:TPU:1 now
where the time goes in v1:
time: 26.1 us; the launch traced here: 25.8 us
  Pallas kernels  23 us (88%)
  local copies, waits for them, and re-layouts  2.79 us (11%)
    pallas_call x1, Pallas kernels, shards(): pl.pallas_call(functools.partial(kernel, n_chan, n_tm), out_shape=jax.Sha...  23 us
    unnamed x2, local copies, waits for them, and re-layouts  2.79 us

profile of v1, /device:TPU:1, one launch (start us, length us, event | category | flops | bytes accessed | tf_op | source)
XLA Modules:
  0.0 25.8 jit_solution(2122903368802390652)
XLA Ops:
  0.0 1.4 %copy.6.shifts = s32[128,16]{1,0:T(8,128)} copy(s32[128,16]{0,1:T(8,128)} %param.8) | data formatting | bytes 16384 | tf_op args[3]
  1.4 23.0 %matched_stack.1 = f32[16,512]{1,0:T(8,128)} custom-call(bf16[16,512]{1,0:T(8,128)(2,1)} %record.1, bf16[16,255]{1,0:T(8,128)(2,1)} %tail.1, bf16[128,16,128]{2,1,0:T(8,128)(2,1)} %templates.1, s32[128,16]{1,0:T(8,128)} %copy.6.shifts, s32[16]{0:T(128)} %mask.1), custom_call_target="tpu_custom_call" | custom-call | tf_op jit(solution)/shard_map/matched_stack/pallas_call | solution.py:185
  24.5 1.4 %copy.8 = f32[16,512]{1,0:T(8,128)} copy(f32[16,512]{1,0:T(8,128)} %matched_stack.1) | data formatting | bytes 65536

commit v2 on v1

v2 whole, which is shorter than its diff:
```python
import functools

import jax
import jax.numpy as jnp
from jax import lax
from jax.experimental import pallas as pl
from jax.experimental.pallas import tpu as pltpu
from jax.sharding import PartitionSpec as P

MESH = pl.DeviceIdType.MESH
LANES = 128
SUBLANES = 8
WIRE = jnp.float32
NORM_UNROLL = 2
CORR_UNROLL = 8


def ahead(values, distance):
    width = values.shape[1]
    distance = distance % width
    if distance == 0:
        return values
    return pltpu.roll(values, width - distance, 1)


def hankel(samples, tap_count, lag_count):
    width = samples.shape[1]
    rows = jnp.broadcast_to(samples, (SUBLANES, width))
    row = lax.broadcasted_iota(jnp.int32, (SUBLANES, width), 0)
    for bit in range(3):
        rows = jnp.where((row >> bit) & 1 == 1, ahead(rows, 1 << bit), rows)
    groups = [ahead(rows, start)[:, :lag_count] for start in range(0, tap_count, SUBLANES)]
    return jnp.concatenate(groups, axis=0).astype(jnp.bfloat16)


def kernel(n_chan, n_tm, record_in, tail_in, templates_in, shifts_in, mask_in, out, record, tail, templates, shifts,
           mask, ext, halo, inverse, unit, positions, normed, part, landed, tally, tallies,
           load_sem, send_sem, recv_sem, tally_send, tally_recv, halo_send, halo_recv):
    chan = lax.axis_index("chan")
    tm = lax.axis_index("tm")
    chan_count, out_len = record.shape
    templ_count, _, tap_count = templates.shape
    halo_len = tail.shape[1]
    halo_width = halo.shape[1]
    rows = templ_count // n_chan
    early = out_len - LANES
    f32 = jnp.float32

    barrier = pltpu.get_barrier_semaphore()

    @pl.when(tm > 0)
    def _():
        pl.semaphore_signal(barrier, inc=1, device_id={"tm": tm - 1}, device_id_type=MESH)

    @pl.when(tm < n_tm - 1)
    def _():
        pl.semaphore_signal(barrier, inc=1, device_id={"tm": tm + 1}, device_id_type=MESH)

    for i in range(1, n_chan):
        pl.semaphore_signal(barrier, inc=1, device_id={"chan": lax.rem(chan + i, n_chan)}, device_id_type=MESH)

    pairs = ((record_in, record), (shifts_in, shifts), (templates_in, templates), (mask_in, mask), (tail_in, tail))
    record_load, shifts_load, templates_load, mask_load, tail_load = [
        pltpu.make_async_copy(source, place, load_sem.at[i]) for i, (source, place) in enumerate(pairs)]
    for load in (record_load, shifts_load, templates_load, mask_load, tail_load):
        load.start()

    record_load.wait()
    ext[:, :out_len] = record[...].astype(f32)

    shifts_load.wait()
    channel = lax.broadcasted_iota(jnp.int32, (chan_count, chan_count * LANES), 0)
    owner = lax.broadcasted_iota(jnp.int32, (chan_count, chan_count * LANES), 1) // LANES
    spreader = jnp.where(channel == owner, 1.0, 0.0).astype(jnp.bfloat16)
    moveouts = lax.dot_general(shifts[...].astype(f32).astype(jnp.bfloat16), spreader, (((0,), (0,)), ((), ())),
                               preferred_element_type=f32)
    lane = lax.broadcasted_iota(jnp.int32, (templ_count, chan_count * LANES), 1) & (LANES - 1)
    positions[...] = moveouts.astype(jnp.int32) + lane

    mask_load.wait()
    count = mask[0]
    for c in range(1, chan_count):
        count = count + mask[c]
    tally[...] = jnp.full(tally.shape, count, jnp.int32).astype(f32)

    neighbours = jnp.minimum(tm, 1) + jnp.minimum(n_tm - 1 - tm, 1)
    pl.semaphore_wait(barrier, n_chan - 1 + neighbours)

    halo_copy = pltpu.make_async_remote_copy(
        src_ref=record.at[:, pl.ds(0, halo_width)], dst_ref=halo, send_sem=halo_send, recv_sem=halo_recv,
        device_id={"tm": jnp.maximum(tm - 1, 0)}, device_id_type=MESH)

    def tally_copy(i):
        return pltpu.make_async_remote_copy(
            src_ref=tally, dst_ref=tallies.at[i], send_sem=tally_send.at[i], recv_sem=tally_recv.at[i],
            device_id={"chan": lax.rem(chan + i, n_chan)}, device_id_type=MESH)

    def part_copy(i):
        return pltpu.make_async_remote_copy(
            src_ref=part.at[i], dst_ref=landed.at[i], send_sem=send_sem.at[i], recv_sem=recv_sem.at[i],
            device_id={"chan": lax.rem(chan + i, n_chan)}, device_id_type=MESH)

    @pl.when(tm > 0)
    def _():
        halo_copy.start()

    for i in range(1, n_chan):
        tally_copy(i).start()

    templates_load.wait()
    group = min(16, templ_count)

    def normalise(i, carry):
        values = templates[pl.ds(i * group, group)].astype(f32).reshape(group * chan_count, tap_count)
        centered = values - jnp.sum(values, axis=1, keepdims=True) * (1.0 / tap_count)
        power = jnp.sum(centered * centered, axis=1, keepdims=True) * (1.0 / tap_count)
        scale = 1.0 / jnp.sqrt(tap_count * (power + 1e-06))
        unit[pl.ds(pl.multiple_of(i * group * chan_count, SUBLANES), group * chan_count), :] = centered * scale
        return carry

    lax.fori_loop(0, templ_count // group, normalise, 0, unroll=NORM_UNROLL)

    def correlate_span(start, width):
        lags = width - tap_count
        sums = ext[:, start:start + width]
        squares = sums * sums
        for bit in range(tap_count.bit_length() - 1):
            sums = sums + ahead(sums, 1 << bit)
            squares = squares + ahead(squares, 1 << bit)
        window = sums[:, :lags]
        variance = jnp.maximum(squares[:, :lags] - window * window * (1.0 / tap_count), 0.0)
        inverse[:, start:start + lags] = 1.0 / jnp.sqrt(variance + tap_count * 1e-06)

        def correlate(c, carry):
            taps = unit[pl.ds(c, templ_count, stride=chan_count), :].astype(jnp.bfloat16)
            product = jnp.dot(taps, hankel(ext[pl.ds(c, 1), start:start + width], tap_count, lags),
                              preferred_element_type=f32)
            weight = jnp.full((1, lags), mask[c], jnp.int32).astype(f32)
            normed[c, :, start:start + lags] = product * (inverse[pl.ds(c, 1), start:start + lags] * weight)
            return carry

        lax.fori_loop(0, chan_count, correlate, 0, unroll=CORR_UNROLL)

    correlate_span(0, out_len)
    tail_load.wait()

    @pl.when(tm < n_tm - 1)
    def _():
        halo_copy.wait_recv()
        ext[:, out_len:] = halo[...].astype(f32)

    @pl.when(tm == n_tm - 1)
    def _():
        ext[:, out_len:] = jnp.zeros((chan_count, halo_width), f32)
        ext[:, out_len:out_len + halo_len] = tail[...].astype(f32)

    correlate_span(early, LANES + halo_width)

    def block_sum(block):
        place = pl.ds(pl.multiple_of(block * rows, SUBLANES), rows)
        tiles = out_len // LANES
        totals = [jnp.zeros((rows, LANES), f32)] * tiles
        for c in range(chan_count):
            position = positions[place, c * LANES:(c + 1) * LANES]
            index = position & (LANES - 1)
            inside = position < LANES
            turned = [
                jnp.take_along_axis(normed[c, place, pl.ds(b * LANES, LANES)], index, axis=1,
                                    mode="promise_in_bounds")
                for b in range(tiles + 1)
            ]
            totals = [totals[b] + jnp.where(inside, turned[b], turned[b + 1]) for b in range(tiles)]
        return jnp.concatenate(totals, axis=1)

    def ship(i, carry):
        part[i] = block_sum(lax.rem(chan + i, n_chan)).astype(part.dtype)
        part_copy(i).start()
        return carry

    lax.fori_loop(1, n_chan, ship, 0)
    total = block_sum(chan)
    number = tally[...]
    for i in range(1, n_chan):
        tally_copy(i).wait_recv()
        number = number + tallies[i]
    scale = jnp.sqrt(tap_count / jnp.maximum(number[0:1, :], 1.0))
    for i in range(1, n_chan):
        part_copy(i).wait_recv()
        total = total + landed[i].astype(f32)
    for b in range(out_len // LANES):
        span = slice(b * LANES, (b + 1) * LANES)
        out[:, span] = total[:, span] * scale

    for i in range(1, n_chan):
        tally_copy(i).wait_send()
        part_copy(i).wait_send()

    @pl.when(tm > 0)
    def _():
        halo_copy.wait_send()


def shards(n_chan, n_tm, record, tail, templates, shifts, mask):
    chan_count, out_len = record.shape
    templ_count, _, tap_count = templates.shape
    halo_len = tail.shape[1]
    halo_width = -(-halo_len // LANES) * LANES
    lag_count = out_len + LANES
    rows = templ_count // n_chan
    assert tap_count == LANES and halo_len - tap_count < LANES and out_len % LANES == 0 and out_len > LANES
    by_channel = shifts.T
    operands = (record, tail, templates, by_channel, mask)
    f32 = jnp.float32
    dma = pltpu.SemaphoreType.DMA
    return pl.pallas_call(
        functools.partial(kernel, n_chan, n_tm),
        out_shape=pltpu.VMEM((rows, out_len), f32),
        in_specs=[pl.BlockSpec(memory_space=pl.ANY)] * len(operands),
        out_specs=pl.BlockSpec(memory_space=pltpu.VMEM),
        scratch_shapes=[
            pltpu.VMEM(record.shape, record.dtype),
            pltpu.VMEM(tail.shape, tail.dtype),
            pltpu.VMEM(templates.shape, templates.dtype),
            pltpu.VMEM(by_channel.shape, shifts.dtype),
            pltpu.SMEM(mask.shape, mask.dtype),
            pltpu.VMEM((chan_count, out_len + halo_width), f32),
            pltpu.VMEM((chan_count, halo_width), record.dtype),
            pltpu.VMEM((chan_count, lag_count), f32),
            pltpu.VMEM((templ_count * chan_count, tap_count), f32),
            pltpu.VMEM((templ_count, chan_count * LANES), jnp.int32),
            pltpu.VMEM((chan_count, templ_count, lag_count), f32),
            pltpu.VMEM((n_chan, rows, out_len), WIRE),
            pltpu.VMEM((n_chan, rows, out_len), WIRE),
            pltpu.VMEM((SUBLANES, LANES), f32),
            pltpu.VMEM((n_chan, SUBLANES, LANES), f32),
            dma((len(operands),)), dma((n_chan,)), dma((n_chan,)), dma((n_chan,)), dma((n_chan,)), dma, dma,
        ],
        compiler_params=pltpu.CompilerParams(collective_id=0, has_side_effects=True),
        name="matched_stack",
    )(*operands)


def solution(mesh):
    in_specs = (P("chan", "tm"), P("chan", None), P(None, "chan", None), P(None, "chan"), P("chan"))
    body = functools.partial(shards, mesh.shape["chan"], mesh.shape["tm"])
    return jax.shard_map(body, mesh=mesh, in_specs=in_specs, out_specs=P("chan", "tm"), check_vma=False)
```

time: 26.1 us -> 15.4 us (0.59)
  the two profiles are of different devices: /device:TPU:1 before, /device:TPU:0 now
where the time goes in v2:
time: 15.4 us; the launch traced here: 15.1 us
  Pallas kernels  14.5 us (94%)
  local copies, waits for them, and re-layouts  0.62 us (4%)
    pallas_call x1, Pallas kernels, shards(): pl.pallas_call(functools.partial(kernel, n_chan, n_tm), out_shape=pltpu.V...  14.5 us
    unnamed x1, local copies, waits for them, and re-layouts  0.62 us

profile of v2, /device:TPU:0, one launch (start us, length us, event | category | flops | bytes accessed | tf_op | source)
XLA Modules:
  0.0 15.1 jit_solution(5970847857746534355)
XLA Ops:
  0.0 14.5 %matched_stack.1 = f32[16,512]{1,0:T(8,128)S(1)} custom-call(bf16[16,512]{1,0:T(8,128)(2,1)} %record_in.1, bf16[16,255]{1,0:T(8,128)(2,1)} %tail_in.1, bf16[128,16,128]{2,1,0:T(8,128)(2,1)} %templates_in.1, s32[16,128]{1,0:T(8,128)} %bitcast.1, s32[16]{0:T(128)} %mask_in.1), custom_call_target="tpu_custom_call" | custom-call | tf_op jit(solution)/shard_map/matched_stack/pallas_call | solution.py:215
  14.5 0.6 %copy.7 = f32[16,512]{1,0:T(8,128)} copy(f32[16,512]{1,0:T(8,128)S(1)} %matched_stack.1) | data formatting | bytes 65536
